TPU v7x, 8 devices: a whole 2x2x1 slice. The times are simulated.
8 devices in a mesh: dp: 1 (over z), tp: 8 (over x, y, core).
Axes of the slice: x: 2, y: 2, z: 1, core: 2. Of those that a mesh axis runs over, the one named last changes fastest.
Arguments:
- x: bfloat16 [128, 7168], P('dp')
- w_gate: bfloat16 [7168, 18432], P(None, 'tp')
- w_up: bfloat16 [7168, 18432], P(None, 'tp')
- w_down: bfloat16 [18432, 7168], P('tp')
Outputs:
- output: bfloat16 [128, 7168], P('dp')
All inputs are finite; a program needn't handle non-finite values.
Results may differ from a plain program's by a relative error of at most 0.016.
Values are sent between devices in bfloat16 or wider.
A program may use at most 2 GiB of HBM per device.

v0:
```python
import jax
import jax.numpy as jnp
from jax import lax
from jax.sharding import PartitionSpec as P


def solution(mesh):
    def step(x, w_gate, w_up, w_down):
        gate = jnp.dot(x, w_gate, preferred_element_type=jnp.float32)
        up = jnp.dot(x, w_up, preferred_element_type=jnp.float32)
        hidden = (jax.nn.silu(gate) * up).astype(jnp.bfloat16)
        term = jnp.dot(hidden, w_down, preferred_element_type=jnp.float32).astype(jnp.bfloat16)
        return lax.psum(term, "tp")

    return jax.shard_map(
        step,
        mesh=mesh,
        in_specs=(P("dp", None), P(None, "tp"), P(None, "tp"), P("tp", None)),
        out_specs=P("dp", None),
        check_vma=False,
    )
```

profile of v0, /device:TPU:0, one launch (start us, length us, event | category | flops | bytes accessed | tf_op | source)
XLA Modules:
  0.0 108.0 jit_solution(7043710720302153255)
XLA Ops:
  6.5 0.0 copy-start
  6.5 0.0 all-reduce.2.cloned.1.call-start
  6.5 1.5 %copy-done = bf16[128,7168]{1,0:T(8,128)(2,1)S(1)} copy-done((bf16[128,7168]{1,0:T(8,128)(2,1)S(1)}, bf16[128,7168]{1,0:T(8,128)(2,1)}, u32[]{:S(2)}) %copy-start) | copy-done | bytes 1835032
  8.0 13.0 %fusion.2 = f32[128,2304]{1,0:T(8,128)S(1)} fusion(bf16[128,7168]{1,0:T(8,128)(2,1)S(1)} %copy-done, bf16[7168,2304]{1,0:T(8,128)(2,1)} %param.5), kind=kOutput, calls=%fused_computation.4 | convolution fusion | flops 4227858432 | bytes 36044800 | tf_op jit(solution)/shard_map/dot_general | solution.py:9
  21.0 25.6 %convolution_convert_fusion = bf16[128,7168]{1,0:T(8,128)(2,1)} fusion(bf16[2304,7168]{1,0:T(8,128)(2,1)} %param.7, bf16[128,7168]{1,0:T(8,128)(2,1)S(1)} %copy-done, bf16[7168,2304]{1,0:T(8,128)(2,1)} %param.6, f32[128,2304]{1,0:T(8,128)S(1)} %fusion.2), kind=kOutput, calls=%fused_computation | convolution fusion | flops 8458403840 | bytes 70909952 | tf_op jit(solution)/shard_map/dot_general | solution.py:12
  46.6 0.0 all-reduce.2.cloned.1.call-update
  46.6 0.0 copy-start.1
  46.7 51.7 %all-reduce.2.cloned.1.call-done = bf16[128,7168]{1,0:T(8,128)(2,1)} async-done(((bf16[128,7168]{1,0:T(8,128)(2,1)}), bf16[128,7168]{1,0:T(8,128)(2,1)}) %all-reduce.2.cloned.1.call-update) | async-done | bytes 1835024 | tf_op jit(solution)/shard_map/psum | solution.py:13
  98.3 2.8 %copy.6 = bf16[128,7168]{1,0:T(8,128)(2,1)} copy(bf16[128,7168]{1,0:T(8,128)(2,1)} %all-reduce.2.cloned.1.call-done) | data formatting | bytes 3670016
  101.2 0.0 copy-done.1
Async XLA Ops:
  6.5 1.5 %copy-start = (bf16[128,7168]{1,0:T(8,128)(2,1)S(1)}, bf16[128,7168]{1,0:T(8,128)(2,1)}, u32[]{:S(2)}) copy-start(bf16[128,7168]{1,0:T(8,128)(2,1)} %param.4) | copy-start | bytes 5505028
  6.5 91.8 %all-reduce.2.cloned.1.call-start = ((), (), s32[]{:S(2)}) async-start(), calls=%async_computation | async-start | bytes 3670016 | tf_op jit(solution)/shard_map/psum | solution.py:13
  46.6 54.5 %copy-start.1 = (bf16[128,7168]{1,0:T(8,128)(2,1)S(1)}, bf16[128,7168]{1,0:T(8,128)(2,1)}, u32[]{:S(2)}) copy-start(bf16[128,7168]{1,0:T(8,128)(2,1)} %param.4) | copy-start | bytes 5505028
Sparse Core Ops, SparseCore 0:
  46.8 51.5 all-reduce.1
where the time goes:
time: 108 us
  waiting for transfers between devices  51.7 us (48%)
  matrix products  38.6 us (36%)
  between operations  13.4 us (12%)
  local copies, waits for them, and re-layouts  4.35 us (4%)
    psum x1, waiting for transfers between devices, step(): return lax.psum(term, 'tp')  51.7 us
    dot_general x1, matrix products, step(): jnp.dot(hidden, w_down, preferred_element_type=jnp.float32)  25.6 us
    dot_general x1, matrix products, step(): gate = jnp.dot(x, w_gate, preferred_element_type=jnp.float32)  13 us
    unnamed x5, local copies, waits for them, and re-layouts  4.35 us
  transfers between devices with their start and end apart: 1, of which 1 were waited for; matrix products, arithmetic and copies ran while one was open for 0% of the time, Pallas kernels for 0%

commit v1 on v0

v1 whole, which is shorter than its diff:
```python
import functools

import jax
import jax.numpy as jnp
from jax import lax
from jax.experimental import pallas as pl
from jax.experimental.pallas import tpu as pltpu
from jax.sharding import PartitionSpec as P

BF = 256
SL = 2
KS = 4
NC = 512
LAGS = (1, 4, 7, 10, 13, 15)


def kernel(x_hbm, wg, wu, wd, y, xv, gb, ub, db, h, t, out, sa, ra, sb, rb, sc, rc,
           xs, gs, us, ds, ys, s1, r1, s2, r2):
    rows, d = xv.shape
    ff = h.shape[1]
    nf, nch, kb, hc = ff // BF, d // NC, d // KS, NC // 2
    me = lax.axis_index("tp")
    core, yb, xb = me % 2, (me // 2) % 2, me // 4
    mate, ynb, xnb = me + 1 - 2 * core, me + 2 - 4 * yb, me + 4 - 8 * xb
    first, second = (xnb, ynb), (ynb, xnb)
    fb, sbit = (xb, yb), (yb, xb)

    barrier = pltpu.get_barrier_semaphore()
    for other in (mate, ynb, xnb):
        pl.semaphore_signal(barrier, inc=1, device_id={"tp": other}, device_id_type=pl.DeviceIdType.MESH)

    def block(f, k):
        s = lax.rem(f, SL)
        src = (pl.ds(k * kb, kb), pl.ds(pl.multiple_of(f * BF, BF), BF))
        dst = (s, pl.ds(k * kb, kb))
        return (pltpu.make_async_copy(wg.at[src], gb.at[dst], gs.at[s, k]),
                pltpu.make_async_copy(wu.at[src], ub.at[dst], us.at[s, k]))

    def down(j):
        return pltpu.make_async_copy(wd.at[:, pl.ds(pl.multiple_of(j * NC, NC), NC)], db.at[j], ds.at[j])

    xcopy = pltpu.make_async_copy(x_hbm, xv, xs)
    xcopy.start()
    for f in range(SL):
        for k in range(KS):
            for c in block(f, k):
                c.start()
    xcopy.wait()

    def hidden(f, carry):
        s = lax.rem(f, SL)
        g = jnp.zeros((rows, BF), jnp.float32)
        u = jnp.zeros((rows, BF), jnp.float32)
        for k in range(KS):
            for c in block(f, k):
                c.wait()
            xk = xv[:, k * kb:(k + 1) * kb]
            g += jnp.dot(xk, gb[s, pl.ds(k * kb, kb)], preferred_element_type=jnp.float32)
            u += jnp.dot(xk, ub[s, pl.ds(k * kb, kb)], preferred_element_type=jnp.float32)
        h[:, pl.ds(pl.multiple_of(f * BF, BF), BF)] = (jax.nn.silu(g) * u).astype(jnp.bfloat16)

        @pl.when(f + SL < nf)
        def _():
            for k in range(KS):
                for c in block(f + SL, k):
                    c.start()

        @pl.when(f + SL == nf)
        def _():
            for j in range(nch):
                down(j).start()

        return carry

    lax.fori_loop(0, nf, hidden, 0)
    pl.semaphore_wait(barrier, 3)

    def remote(src, dst, i, dev):
        return pltpu.make_async_remote_copy(src_ref=src, dst_ref=dst, send_sem=s2.at[i], recv_sem=r2.at[i],
                                            device_id={"tp": dev}, device_id_type=pl.DeviceIdType.MESH)

    def at(n):
        return pl.ds(pl.multiple_of(n, 16), 16)

    def at32(n):
        return pl.ds(pl.multiple_of(n, 32), 32)

    half = core * 64

    def pair(j):
        return pltpu.make_async_remote_copy(src_ref=sa.at[j], dst_ref=ra.at[j], send_sem=s1.at[j], recv_sem=r1.at[j],
                                            device_id={"tp": mate}, device_id_type=pl.DeviceIdType.MESH)

    def send_b(j, c):
        return remote(sb.at[j, c], rb.at[j, c], 8 * j + c, first[c])

    def send_c(j, c):
        return remote(sc.at[j, c], rc.at[j, c], 8 * j + 2 + c, second[c])

    def send_d(j, c):
        r = out.at[j, c, at(half + 32 * fb[c] + 16 * sbit[c])]
        return remote(r, r, 8 * j + 4 + c, second[c])

    def send_e(j, c):
        r = out.at[j, c, at32(half + 32 * fb[c])]
        return remote(r, r, 8 * j + 6 + c, first[c])

    def send_f(j):
        r = out.at[j, :, pl.ds(pl.multiple_of(half, 64), 64)]
        return pltpu.make_async_remote_copy(src_ref=r, dst_ref=r, send_sem=s1.at[nch + j], recv_sem=r1.at[nch + j],
                                            device_id={"tp": mate}, device_id_type=pl.DeviceIdType.MESH)

    def result(j, c):
        cols = pl.ds(pl.multiple_of(j * NC + c * hc, hc), hc)
        return pltpu.make_async_copy(out.at[j, c], y.at[:, cols], ys.at[j, c])

    def matmul(j):
        down(j).wait()
        p = jnp.dot(h[...], db[j], preferred_element_type=jnp.float32)
        for c in range(2):
            t[j, c] = p[:, c * hc:(c + 1) * hc]
        for c in range(2):
            sa[j, c] = t[j, c, pl.ds(pl.multiple_of(64 - half, 64), 64)].astype(jnp.bfloat16)
        pair(j).start()

    def after_a(j):
        pair(j).wait_recv()
        for c in range(2):
            o = 32 * (1 - fb[c])
            v = t[j, c, at32(half + o)] + ra[j, c, at32(o)].astype(jnp.float32)
            sb[j, c] = v.astype(jnp.bfloat16)
            send_b(j, c).start()

    def after_b(j):
        for c in range(2):
            send_b(j, c).wait_recv()
            o = 16 * (1 - sbit[c])
            w = 32 * fb[c] + o
            v = t[j, c, at(half + w)] + ra[j, c, at(w)].astype(jnp.float32)
            v += rb[j, c, at(o)].astype(jnp.float32)
            sc[j, c] = v.astype(jnp.bfloat16)
            send_c(j, c).start()

    def after_c(j):
        for c in range(2):
            send_c(j, c).wait_recv()
            o = 16 * sbit[c]
            w = 32 * fb[c] + o
            v = t[j, c, at(half + w)] + ra[j, c, at(w)].astype(jnp.float32)
            v += rb[j, c, at(o)].astype(jnp.float32)
            v += rc[j, c].astype(jnp.float32)
            out[j, c, at(half + w)] = v.astype(jnp.bfloat16)
            send_d(j, c).start()

    def after_d(j):
        for c in range(2):
            send_d(j, c).wait_recv()
            send_e(j, c).start()

    def after_e(j):
        for c in range(2):
            send_e(j, c).wait_recv()
        send_f(j).start()

    def after_f(j):
        send_f(j).wait_recv()
        for c in range(2):
            result(j, c).start()

    stages = (after_a, after_b, after_c, after_d, after_e, after_f)

    def turn(i, carry):
        @pl.when(i < nch)
        def _():
            matmul(i)

        for lag, stage in zip(LAGS, stages):
            @pl.when(jnp.logical_and(i >= lag, i < nch + lag))
            def _(lag=lag, stage=stage):
                stage(i - lag)

        return carry

    lax.fori_loop(0, nch + LAGS[-1], turn, 0)

    def drain(j, carry):
        pair(j).wait_send()
        for c in range(2):
            for send in (send_b, send_c, send_d, send_e):
                send(j, c).wait_send()
            result(j, c).wait()
        send_f(j).wait_send()
        return carry

    lax.fori_loop(0, nch, drain, 0)


def solution(mesh):
    def step(x, w_gate, w_up, w_down):
        rows, d = x.shape
        ff = w_gate.shape[1]
        nch, hc = d // NC, NC // 2
        bf16, dma = jnp.bfloat16, pltpu.SemaphoreType.DMA
        anywhere = pl.BlockSpec(memory_space=pl.ANY)
        return pl.pallas_call(
            kernel,
            out_shape=jax.ShapeDtypeStruct((rows, d), bf16),
            in_specs=[anywhere] * 4,
            out_specs=anywhere,
            scratch_shapes=[
                pltpu.VMEM((rows, d), bf16),
                pltpu.VMEM((SL, d, BF), bf16),
                pltpu.VMEM((SL, d, BF), bf16),
                pltpu.VMEM((nch, ff, NC), bf16),
                pltpu.VMEM((rows, ff), bf16),
                pltpu.VMEM((nch, 2, rows, hc), jnp.float32),
                pltpu.VMEM((nch, 2, rows, hc), bf16),
                pltpu.VMEM((nch, 2, rows // 2, hc), bf16),
                pltpu.VMEM((nch, 2, rows // 2, hc), bf16),
                pltpu.VMEM((nch, 2, rows // 4, hc), bf16),
                pltpu.VMEM((nch, 2, rows // 4, hc), bf16),
                pltpu.VMEM((nch, 2, rows // 8, hc), bf16),
                pltpu.VMEM((nch, 2, rows // 8, hc), bf16),
                dma,
                dma((SL, KS)),
                dma((SL, KS)),
                dma((nch,)),
                dma((nch, 2)),
                dma((2 * nch,)),
                dma((2 * nch,)),
                dma((8 * nch,)),
                dma((8 * nch,)),
            ],
            compiler_params=pltpu.CompilerParams(
                collective_id=0, has_side_effects=True, vmem_limit_bytes=67043328
            ),
        )(x, w_gate, w_up, w_down)

    return jax.shard_map(
        step,
        mesh=mesh,
        in_specs=(P("dp", None), P(None, "tp"), P(None, "tp"), P("tp", None)),
        out_specs=P("dp", None),
        check_vma=False,
    )
```

time: 108 us -> 58.1 us (0.54)
  Pallas kernels: 0 us -> 55 us
  waiting for transfers between devices: 51.7 us -> 0 us
  matrix products: 38.6 us -> 0 us
  between operations: 13.4 us -> 0.01 us
  local copies, waits for them, and re-layouts: 4.35 us -> 2.85 us
    pallas_call x0 -> x1, Pallas kernels: none -> 55 us  [step(): pl.pallas_call(kernel, out_shape=jax.ShapeDtypeStruct((rows, d), bf16), i...]
    psum x1 -> x0, waiting for transfers between devices: 51.7 us -> none  [step(): return lax.psum(term, 'tp')]
    dot_general x2 -> x0, matrix products: 38.6 us -> none  [the longest x1 25.6 us: step(): jnp.dot(hidden, w_down, preferred_element_type=jnp.float32)]
    unnamed x5 -> x1, local copies, waits for them, and re-layouts: 4.35 us -> 2.85 us
  transfers between devices with their start and end apart: 1 -> 0, of which waited for: 1 -> 0; matrix products, arithmetic and copies ran while one was open for 0% -> 0% of each run, Pallas kernels for 0% -> 0%
where the time goes in v1:
time: 58.1 us; the launch traced here: 57.8 us
  Pallas kernels  55 us (95%)
  local copies, waits for them, and re-layouts  2.85 us (5%)
    pallas_call x1, Pallas kernels, step(): pl.pallas_call(kernel, out_shape=jax.ShapeDtypeStruct((rows, d), bf16), i...  55 us
    unnamed x1, local copies, waits for them, and re-layouts  2.85 us

profile of v1, /device:TPU:0, one launch (start us, length us, event | category | flops | bytes accessed | tf_op | source)
XLA Modules:
  0.0 57.8 jit_solution(1784963235322261213)
XLA Ops:
  0.0 55.0 %shard_map.46 = bf16[128,7168]{1,0:T(8,128)(2,1)} custom-call(bf16[128,7168]{1,0:T(8,128)(2,1)} %x_hbm.1, bf16[7168,2304]{1,0:T(8,128)(2,1)} %wg.1, bf16[7168,2304]{1,0:T(8,128)(2,1)} %wu.1, bf16[2304,7168]{1,0:T(8,128)(2,1)} %wd.1), custom_call_target="tpu_custom_call" | custom-call | tf_op jit(solution)/shard_map/pallas_call | solution.py:205
  55.0 2.8 %copy.6 = bf16[128,7168]{1,0:T(8,128)(2,1)} copy(bf16[128,7168]{1,0:T(8,128)(2,1)} %shard_map.46) | data formatting | bytes 3670016
